TPU v7x, 32 devices: a whole 2x2x4 slice. The times are simulated.
32 devices in a mesh: fsdp: 4 (over y, x), tenant: 4 (over z), dp: 2 (over core).
Axes of the slice: x: 2, y: 2, z: 4, core: 2. Of those that a mesh axis runs over, the one named last changes fastest.
Arguments:
- tokens: bfloat16 [3072, 5120], P(('fsdp', 'dp'), 'tenant'), may hold values from -6 to 6
- block_tenant_index: int32 [48], P(('fsdp', 'dp')), may hold values from 0 to 7
- ranks: int32 [8], replicated, may hold values from 16 to 64, as said below
- frozen_up_weight: bfloat16 [5120, 14336], P(('fsdp', 'dp'), 'tenant'), may hold values from -0.078125 to 0.078125
- tenant_down_adapters: bfloat16 [8, 64, 5120], P('tenant'), may hold values from -0.078125 to 0.078125
- tenant_up_adapters: bfloat16 [8, 64, 14336], P('tenant'), may hold values from -0.75 to 0.75
- cotangent: bfloat16 [3072, 14336], P(('fsdp', 'dp'), 'tenant'), may hold values from -6 to 6
Outputs:
- hidden_out: bfloat16 [3072, 14336], P(('fsdp', 'dp'), 'tenant')
- grad_tokens: bfloat16 [3072, 5120], P(('fsdp', 'dp'), 'tenant')
- grad_down: float32 [8, 64, 5120], P('dp', None, 'tenant')
- grad_up: float32 [8, 64, 14336], P('dp', None, 'tenant')
Inputs may be any that keep to these rules, and one draw needn't show every extreme that they name: `ranks`: multiples of 16; some tenant has rank 64.
All inputs are finite; a program needn't handle non-finite values.
Results may differ from a plain program's by a relative error of at most 0.0034.
Values may be sent and summed in bfloat16 or wider, within the bound.
A program may use at most 128 MiB of HBM per device.

v0:
```python
import jax
import jax.numpy as jnp
from jax import lax
from jax.sharding import PartitionSpec as P

BLOCK = 64
alpha_scale = 32.0
BF16 = jnp.bfloat16
F32 = jnp.float32


def nt(a, b):
    return lax.dot_general(a, b, (((1,), (1,)), ((), ())), preferred_element_type=F32)


def tn(a, b):
    return lax.dot_general(a, b, (((0,), (0,)), ((), ())), preferred_element_type=F32)


def fetch_adapter(adapter, tenant_n, dp_n):
    share = adapter.shape[1] // dp_n
    mine = lax.dynamic_slice_in_dim(adapter, lax.axis_index("dp") * share, share, axis=1)
    part = lax.all_to_all(mine, "tenant", split_axis=2, concat_axis=0, tiled=True)
    return lax.all_gather(part, "dp", axis=1, tiled=True)


def reduce_fsdp(x, fsdp_n):
    rows = x.shape[0]
    got = lax.all_to_all(
        x.astype(BF16).reshape(fsdp_n, rows // fsdp_n, x.shape[1]), "fsdp", 0, 0, tiled=True
    )
    total = jnp.sum(got.astype(F32), axis=0).astype(BF16)
    return lax.all_gather(total, "fsdp", axis=0, tiled=True).astype(F32)


def make_shards(mesh):
    tenant_n, fsdp_n, dp_n = (mesh.shape["tenant"], mesh.shape["fsdp"], mesh.shape["dp"])

    def shards(
        tokens,
        block_tenant_index,
        ranks,
        frozen_up_weight,
        tenant_down_adapters,
        tenant_up_adapters,
        cotangent,
    ):
        rows, local_d = tokens.shape
        local_f = cotangent.shape[1]
        tenants = ranks.shape[0]
        rank = tenant_down_adapters.shape[1]
        depth = frozen_up_weight.shape[0]
        blocks = fsdp_n * dp_n
        first = max(128, depth * 3 // 5 // 128 * 128) if depth > 128 else depth
        cuts = [(0, first)] + ([(first, depth)] if first < depth else [])
        weights = [
            lax.all_gather(frozen_up_weight[a:b], ("fsdp", "dp"), axis=0, tiled=True)
            for a, b in cuts
        ]
        up = fetch_adapter(tenant_up_adapters, tenant_n, dp_n).reshape(tenants * rank, local_f)
        down = fetch_adapter(tenant_down_adapters, tenant_n, dp_n).reshape(tenants * rank, local_d)
        onehot = block_tenant_index[:, None] == jnp.arange(tenants, dtype=jnp.int32)[None, :]
        sel = onehot.astype(F32)[:, None, :, None]
        own_rank = jnp.sum(jnp.where(onehot, ranks[None, :], 0), axis=1)
        keep = jnp.arange(rank, dtype=jnp.int32)[None, :] < own_rank[:, None]
        gain = jnp.where(keep, (alpha_scale / own_rank.astype(F32))[:, None], F32(0.0))

        def compact(full):
            full = full.reshape(rows // BLOCK, BLOCK, tenants, rank)
            return jnp.sum(full * sel, axis=2)

        both = jnp.concatenate([compact(nt(tokens, down)), compact(nt(cotangent, up))], axis=2)
        both = lax.psum(both, "tenant")

        def spread(values):
            scaled = (values * gain[:, None, :]).astype(BF16)
            return (scaled[:, :, None, :] * sel.astype(BF16)).reshape(rows, tenants * rank)

        adapted = spread(both[:, :, :rank])
        adapted_grad = spread(both[:, :, rank:])
        terms = jnp.concatenate([tn(adapted, cotangent), tn(adapted_grad, tokens)], axis=1)
        terms = lax.psum_scatter(terms, "dp", scatter_dimension=0, tiled=True)
        grads = reduce_fsdp(terms, fsdp_n)
        grad_up = grads[:, :local_f].reshape(tenants // dp_n, rank, local_f)
        grad_down = grads[:, local_f:].reshape(tenants // dp_n, rank, local_d)
        whole = lax.all_gather(tokens, "tenant", axis=1, tiled=True)
        whole3 = whole.reshape(rows, blocks, depth)
        hidden = jnp.dot(adapted, up, preferred_element_type=F32)
        pieces = []
        for (a, b), weight in zip(cuts, weights):
            back = nt(cotangent, weight).astype(BF16)
            n = b - a
            got = lax.all_to_all(
                back.reshape(rows, tenant_n, blocks * n // tenant_n).transpose(1, 0, 2),
                "tenant",
                0,
                0,
                tiled=True,
            )
            pieces.append(jnp.sum(got.astype(F32), axis=0).reshape(rows, blocks // tenant_n, n))
            hidden = hidden + jnp.dot(
                whole3[:, :, a:b].reshape(rows, blocks * n), weight, preferred_element_type=F32
            )
        hidden_out = hidden.astype(BF16)
        grad_base = jnp.concatenate(pieces, axis=2).reshape(rows, local_d)
        grad_tokens = (grad_base + jnp.dot(adapted_grad, down, preferred_element_type=F32)).astype(
            BF16
        )
        return (hidden_out, grad_tokens, grad_down, grad_up)

    return shards


def solution(mesh):
    return jax.shard_map(
        make_shards(mesh),
        mesh=mesh,
        in_specs=(
            P(("fsdp", "dp"), "tenant"),
            P(("fsdp", "dp")),
            P(),
            P(("fsdp", "dp"), "tenant"),
            P("tenant", None, None),
            P("tenant", None, None),
            P(("fsdp", "dp"), "tenant"),
        ),
        out_specs=(
            P(("fsdp", "dp"), "tenant"),
            P(("fsdp", "dp"), "tenant"),
            P("dp", None, "tenant"),
            P("dp", None, "tenant"),
        ),
        check_vma=False,
    )
```

profile of v0, /device:TPU:0, one launch (start us, length us, event | category | flops | bytes accessed | tf_op | source)
XLA Modules:
  0.0 595.5 jit_solution(8852192433115120866)
XLA Ops:
  8.5 4.0 copy.30
  12.5 4.9 reshape.171
  17.4 6.3 %all-to-all-start = ((bf16[4,2,40960]{2,1,0:T(2,128)(2,1)}), bf16[4,2,40960]{2,1,0:T(2,128)(2,1)S(1)}, u32[]{:S(2)}, u32[]{:S(2)}) async-start(bf16[4,2,40960]{2,1,0:T(2,128)(2,1)} %reshape.171), calls=%async_computation | async-start | bytes 1310720 | tf_op jit(solution)/shard_map/all_to_all | solution.py:23
  23.8 2.8 constant_dynamic-slice_fusion
  26.6 15.2 %copy.31 = bf16[2,32,14336]{1,0,2:T(2,128)(2,1)} copy(bf16[2,32,14336]{2,1,0:T(8,128)(2,1)} %constant_dynamic-slice_fusion) | data formatting | bytes 3670016
  41.9 9.4 %reshape.173 = bf16[4,2,114688]{2,1,0:T(2,128)(2,1)} reshape(bf16[14336,2,32]{2,1,0:T(2,128)(2,1)} %bitcast.65) | data formatting | bytes 3670016
  51.3 5.1 all-to-all-start.1
  56.4 2.6 reshape.172
  59.0 6.2 %copy.28 = bf16[2,32,4,1280]{3,2,1,0:T(4,128)(2,1)S(1)} copy(bf16[2,32,4,1280]{1,0,3,2:T(2,128)(2,1)} %bitcast.70) | data formatting | bytes 1310720 | tf_op jit(solution)/shard_map/all_to_all | solution.py:23
  66.2 32.3 %all-to-all-done.1 = bf16[4,2,114688]{2,1,0:T(2,128)(2,1)} async-done(((bf16[4,2,114688]{2,1,0:T(2,128)(2,1)}), bf16[4,2,114688]{2,1,0:T(2,128)(2,1)}, u32[]{:S(2)}, u32[]{:S(2)}) %all-to-all-start.1) | async-done | bytes 1835040 | tf_op jit(solution)/shard_map/all_to_all | solution.py:23
  98.5 6.9 %reshape.174 = bf16[14336,2,32]{2,1,0:T(2,128)(2,1)} reshape(bf16[4,2,114688]{2,1,0:T(2,128)(2,1)} %all-to-all-done.1) | data formatting | bytes 3670016
  105.4 18.1 %copy.29 = bf16[2,32,4,3584]{3,2,1,0:T(4,128)(2,1)} copy(bf16[2,32,4,3584]{1,0,3,2:T(2,128)(2,1)} %bitcast.66) | data formatting | bytes 3670016 | tf_op jit(solution)/shard_map/all_to_all | solution.py:23
  123.5 3.0 copy.24
  126.7 3.3 convolution_bitcast_fusion.1
  132.9 5.8 all-gather.9.cloned.1.call-done
  138.7 5.0 convolution_bitcast_fusion
  146.6 2.9 multiply_reduce_fusion.1
  151.4 35.2 %all-reduce.2.cloned.1.call-done = f32[6,64,128]{2,1,0:T(8,128)} async-done(((f32[6,64,128]{2,1,0:T(8,128)}), f32[6,64,128]{2,1,0:T(8,128)}) %all-reduce.2.cloned.1.call-update) | async-done | bytes 196624 | tf_op jit(solution)/shard_map/psum | solution.py:73
  189.2 1.7 mul.91
  190.9 1.8 mul.87
  192.7 3.6 fusion.11
  196.3 5.0 fusion.10
  201.3 8.3 %pad_maximum_fusion = f32[512,4864]{1,0:T(8,128)} fusion(f32[512,1280]{1,0:T(8,128)} %fusion.11, f32[512,3584]{1,0:T(8,128)} %fusion.10), kind=kLoop, calls=%fused_computation | loop fusion | flops 2490368 | bytes 19922944 | tf_op jit(solution)/shard_map/concatenate | solution.py:81
  209.7 2.9 slice.28
  212.6 3.5 slice.26
  216.2 48.0 %all-gather.11.cloned.1.call-done = bf16[384,5120]{1,0:T(8,128)(2,1)} async-done(((bf16[384,1280]{1,0:T(8,128)(2,1)}), bf16[384,5120]{1,0:T(8,128)(2,1)}) %all-gather.11.cloned.1.call-update) | async-done | bytes 3932176 | tf_op jit(solution)/shard_map/all_gather | solution.py:86
  264.2 2.9 copy.34
  267.5 1.9 copy.35
  271.1 11.4 %reduce-scatter.2.cloned.1.call-done = f32[256,4864]{1,0:T(8,128)} async-done(((f32[512,4864]{1,0:T(8,128)}), f32[256,4864]{1,0:T(8,128)}) %reduce-scatter.2.cloned.1.call-update) | async-done | bytes 4980752 | tf_op jit(solution)/shard_map/reduce_scatter | solution.py:82
  282.5 4.1 convert_element_type.69
  286.6 4.6 all-to-all-start.4
  291.2 6.6 %fusion.8 = f32[384,3584]{1,0:T(8,128)} fusion(bf16[384,512]{1,0:T(8,128)(2,1)S(1)} %mul.87, bf16[512,3584]{1,0:T(8,128)(2,1)} %bitcast.82), kind=kOutput, calls=%fused_computation.33 | convolution fusion | flops 1409286144 | bytes 9568256 | tf_op jit(solution)/shard_map/dot_general | solution.py:88
  297.8 92.3 %all-gather.15.cloned.1.call-done = bf16[2048,3584]{1,0:T(8,128)(2,1)} async-done(((bf16[256,3584]{1,0:T(8,128)(2,1)}), bf16[2048,3584]{1,0:T(8,128)(2,1)}) %all-gather.15.cloned.1.call-update) | async-done | bytes 14680080 | tf_op jit(solution)/shard_map/all_gather | solution.py:57
  390.1 9.4 %convolution_convert_fusion.1 = bf16[384,2048]{1,0:T(8,128)(2,1)S(1)} fusion(bf16[384,3584]{1,0:T(8,128)(2,1)S(1)} %copy-done, bf16[2048,3584]{1,0:T(8,128)(2,1)} %all-gather.15.cloned.1.call-done), kind=kOutput, calls=%fused_computation.9 | convolution fusion | flops 5637931008 | bytes 19005440 | tf_op jit(solution)/shard_map/dot_general | solution.py:13
  400.9 4.6 all-to-all-start.3
  405.5 3.1 reduce_sum.62
  408.6 95.9 %all-gather.13.cloned.1.call-done = bf16[3072,3584]{1,0:T(8,128)(2,1)} async-done(((bf16[384,3584]{1,0:T(8,128)(2,1)}), bf16[3072,3584]{1,0:T(8,128)(2,1)}) %all-gather.13.cloned.1.call-update) | async-done | bytes 22020112 | tf_op jit(solution)/shard_map/all_gather | solution.py:57
  504.5 14.0 %convolution_convert_fusion = bf16[384,3072]{1,0:T(8,128)(2,1)} fusion(bf16[384,3584]{1,0:T(8,128)(2,1)S(1)} %copy-done, bf16[3072,3584]{1,0:T(8,128)(2,1)} %all-gather.13.cloned.1.call-done), kind=kOutput, calls=%fused_computation.5 | convolution fusion | flops 8456896512 | bytes 27131904 | tf_op jit(solution)/shard_map/dot_general | solution.py:13
  518.6 3.2 copy.40
  521.8 4.7 all-to-all-start.2
  526.5 11.6 %fusion.9 = f32[384,3584]{1,0:T(8,128)} fusion(bf16[384,2048]{1,0:T(8,128)(2,1)S(1)} %bitcast.87, bf16[2048,3584]{1,0:T(8,128)(2,1)} %all-gather.15.cloned.1.call-done), kind=kOutput, calls=%fused_computation.34 | convolution fusion | flops 5637144576 | bytes 21757952 | tf_op jit(solution)/shard_map/dot_general | solution.py:101
  541.2 4.2 all-gather.17.cloned.1.call-done
  545.4 2.4 slice.36
  547.8 2.3 slice.37
  550.1 18.7 %fusion.1 = bf16[384,3584]{1,0:T(8,128)(2,1)} fusion(f32[384,3584]{1,0:T(8,128)} %fusion.9, f32[384,3584]{1,0:T(8,128)} %fusion.8, bf16[384,3072]{1,0:T(8,128)(2,1)S(1)} %bitcast.85, bf16[3072,3584]{1,0:T(8,128)(2,1)} %all-gather.13.cloned.1.call-done), kind=kOutput, calls=%fused_computation.3 | convolution fusion | flops 8459845632 | bytes 38141952 | tf_op jit(solution)/shard_map/dot_general | solution.py:101
  568.8 12.2 %all-to-all-done.2 = bf16[4,384,768]{2,1,0:T(8,128)(2,1)} async-done(((bf16[4,384,768]{2,1,0:T(8,128)(2,1)}), bf16[4,384,768]{2,1,0:T(8,128)(2,1)}, u32[]{:S(2)}, u32[]{:S(2)}) %all-to-all-start.2) | async-done | bytes 2359328 | tf_op jit(solution)/shard_map/all_to_all | solution.py:93
  581.0 2.1 convert_reduce_fusion
  583.8 2.0 pad_maximum_fusion.1
  (58 shorter events, 22.7 us)
Async XLA Ops:
  7.2 131.6 %copy-start = (bf16[384,3584]{1,0:T(8,128)(2,1)S(1)}, bf16[384,3584]{1,0:T(8,128)(2,1)}, u32[]{:S(2)}) copy-start(bf16[384,3584]{1,0:T(8,128)(2,1)} %param.13) | copy-start | bytes 8257540
  17.4 33.8 %all-to-all-start = ((bf16[4,2,40960]{2,1,0:T(2,128)(2,1)}), bf16[4,2,40960]{2,1,0:T(2,128)(2,1)S(1)}, u32[]{:S(2)}, u32[]{:S(2)}) async-start(bf16[4,2,40960]{2,1,0:T(2,128)(2,1)} %reshape.171), calls=%async_computation | async-start | bytes 1310720 | tf_op jit(solution)/shard_map/all_to_all | solution.py:23
  51.3 47.2 %all-to-all-start.1 = ((bf16[4,2,114688]{2,1,0:T(2,128)(2,1)}), bf16[4,2,114688]{2,1,0:T(2,128)(2,1)}, u32[]{:S(2)}, u32[]{:S(2)}) async-start(bf16[4,2,114688]{2,1,0:T(2,128)(2,1)} %reshape.173), calls=%async_computation.1 | async-start | bytes 3670016 | tf_op jit(solution)/shard_map/all_to_all | solution.py:23
  56.4 70.4 %all-gather.7.cloned.1.call-start = ((), (), s32[]{:S(2)}) async-start(), calls=%async_computation.6 | async-start | bytes 1966080 | tf_op jit(solution)/shard_map/all_gather | solution.py:24
  66.1 72.6 %all-gather.9.cloned.1.call-start = ((), (), s32[]{:S(2)}) async-start(), calls=%async_computation.7 | async-start | bytes 5505024 | tf_op jit(solution)/shard_map/all_gather | solution.py:24
  123.5 3.1 copy-start.6
  126.6 60.1 %all-reduce.2.cloned.1.call-start = ((), (), s32[]{:S(2)}) async-start(), calls=%async_computation.8 | async-start | bytes 393216 | tf_op jit(solution)/shard_map/psum | solution.py:73
  146.6 4.6 copy-start.7
  150.3 113.9 %all-gather.11.cloned.1.call-start = ((), (), s32[]{:S(2)}) async-start(), calls=%async_computation.9 | async-start | bytes 4915200 | tf_op jit(solution)/shard_map/all_gather | solution.py:86
  150.9 131.6 %reduce-scatter.2.cloned.1.call-start = ((), (), s32[]{:S(2)}) async-start(), calls=%async_computation.12 | async-start | bytes 14942208 | tf_op jit(solution)/shard_map/reduce_scatter | solution.py:82
  209.6 180.5 %all-gather.15.cloned.1.call-start = ((), (), s32[]{:S(2)}) async-start(), calls=%async_computation.11 | async-start | bytes 16515072 | tf_op jit(solution)/shard_map/all_gather | solution.py:57
  212.6 291.9 %all-gather.13.cloned.1.call-start = ((), (), s32[]{:S(2)}) async-start(), calls=%async_computation.10 | async-start | bytes 24772608 | tf_op jit(solution)/shard_map/all_gather | solution.py:57
  286.6 114.2 %all-to-all-start.4 = ((bf16[4,64,4864]{2,1,0:T(8,128)(2,1)}), bf16[4,64,4864]{2,1,0:T(8,128)(2,1)}, u32[]{:S(2)}, u32[]{:S(2)}) async-start(bf16[4,64,4864]{2,1,0:T(8,128)(2,1)} %bitcast.71), calls=%async_computation.5 | async-start | bytes 4980736 | tf_op jit(solution)/shard_map/all_to_all | solution.py:29
  400.9 120.9 %all-to-all-start.3 = ((bf16[4,384,512]{2,1,0:T(8,128)(2,1)}), bf16[4,384,512]{2,1,0:T(8,128)(2,1)}, u32[]{:S(2)}, u32[]{:S(2)}) async-start(bf16[4,384,512]{2,1,0:T(8,128)(2,1)} %bitcast.77), calls=%async_computation.3 | async-start | bytes 3145728 | tf_op jit(solution)/shard_map/all_to_all | solution.py:93
  405.5 139.9 %all-gather.17.cloned.1.call-start = ((), (), s32[]{:S(2)}) async-start(), calls=%async_computation.13 | async-start | bytes 3112960 | tf_op jit(solution)/shard_map/all_gather | solution.py:33
  521.8 4.7 copy-start.4
  521.8 59.2 %all-to-all-start.2 = ((bf16[4,384,768]{2,1,0:T(8,128)(2,1)}), bf16[4,384,768]{2,1,0:T(8,128)(2,1)}, u32[]{:S(2)}, u32[]{:S(2)}) async-start(bf16[4,384,768]{2,1,0:T(8,128)(2,1)} %bitcast.62), calls=%async_computation.2 | async-start | bytes 4718592 | tf_op jit(solution)/shard_map/all_to_all | solution.py:93
  545.4 2.4 copy-start.2
  547.8 2.3 copy-start.3
  585.8 1.3 copy-start.5
  585.8 2.9 copy-start.1
Sparse Core Ops, SparseCore 0:
  66.2 10.8 all-gather.6
  126.7 11.9 all-gather.8
  150.5 36.1 all-reduce.1
  188.1 76.0 all-gather.10
  266.4 16.1 reduce-scatter.1
  284.3 105.8 all-gather.14
  392.6 111.8 all-gather.12
  506.9 38.4 all-gather.16
where the time goes:
time: 598 us; the launch traced here: 596 us
  waiting for transfers between devices  338 us (57%)
  local copies, waits for them, and re-layouts  111 us (19%)
  matrix products  79 us (13%)
  other arithmetic  27.8 us (5%)
  starting transfers between devices  25.8 us (4%)
  between operations  14.3 us (2%)
    all_gather x2, waiting for transfers between devices, shards(): lax.all_gather(frozen_up_weight[a:b], ('fsdp', 'dp'), axis=0, tiled=True)  188 us
    unnamed x26, local copies, waits for them, and re-layouts  51 us
    all_gather x1, waiting for transfers between devices, shards(): whole = lax.all_gather(tokens, 'tenant', axis=1, tiled=True)  48 us
    psum x1, waiting for transfers between devices, shards(): both = lax.psum(both, 'tenant')  35.2 us
    all_to_all x2, waiting for transfers between devices, fetch_adapter(): lax.all_to_all(mine, 'tenant', split_axis=2, concat_axis=0, tiled=True)  32.3 us
    dot_general x4, matrix products, nt(): lax.dot_general(a, b, (((1,), (1,)), ((), ())), preferred_element_type=F32)  31.8 us
    dot_general x2, matrix products, shards(): jnp.dot(whole3[:, :, a:b].reshape(rows, blocks * n), weight, preferred_el...  30.3 us
    all_to_all x4, local copies, waits for them, and re-layouts, fetch_adapter(): lax.all_to_all(mine, 'tenant', split_axis=2, concat_axis=0, tiled=True)  28.3 us
  transfers between devices with their start and end apart: 13, of which 9 were waited for; matrix products, arithmetic and copies ran while one was open for 32% of the time, Pallas kernels for 0%

commit v1 on v0

--- a/solution.py
+++ b/solution.py
@@ -70,7 +70,7 @@
             return jnp.sum(full * sel, axis=2)
 
         both = jnp.concatenate([compact(nt(tokens, down)), compact(nt(cotangent, up))], axis=2)
-        both = lax.psum(both, "tenant")
+        both = jnp.sum(lax.all_gather(both, "tenant"), axis=0)
 
         def spread(values):
             scaled = (values * gain[:, None, :]).astype(BF16)

time: 598 us -> 564 us (0.943)
  waiting for transfers between devices: 338 us -> 273 us
  blocking collectives: 0 us -> 30.7 us
    psum x1 -> x0, waiting for transfers between devices: 35.2 us -> none  [shards(): both = lax.psum(both, 'tenant')]
    all_gather x0 -> x1, blocking collectives: none -> 30.7 us  [shards(): both = jnp.sum(lax.all_gather(both, 'tenant'), axis=0)]
    all_gather x1, waiting for transfers between devices: 48 us -> 19.7 us  [shards(): whole = lax.all_gather(tokens, 'tenant', axis=1, tiled=True)]
  transfers between devices with their start and end apart: 13 -> 12, of which waited for: 9 -> 8; matrix products, arithmetic and copies ran while one was open for 32% -> 36% of each run, Pallas kernels for 0% -> 0%
where the time goes in v1:
time: 564 us; the launch traced here: 562 us
  waiting for transfers between devices  273 us (48%)
  local copies, waits for them, and re-layouts  111 us (20%)
  matrix products  79 us (14%)
  blocking collectives  30.7 us (5%)
  other arithmetic  28 us (5%)
  starting transfers between devices  25.6 us (5%)
  between operations  14.3 us (3%)
    all_gather x2, waiting for transfers between devices, shards(): lax.all_gather(frozen_up_weight[a:b], ('fsdp', 'dp'), axis=0, tiled=True)  188 us
    unnamed x26, local copies, waits for them, and re-layouts  51 us
    all_to_all x2, waiting for transfers between devices, fetch_adapter(): lax.all_to_all(mine, 'tenant', split_axis=2, concat_axis=0, tiled=True)  32.3 us
    dot_general x4, matrix products, nt(): lax.dot_general(a, b, (((1,), (1,)), ((), ())), preferred_element_type=F32)  31.9 us
    all_gather x1, blocking collectives, shards(): both = jnp.sum(lax.all_gather(both, 'tenant'), axis=0)  30.7 us
    dot_general x2, matrix products, shards(): jnp.dot(whole3[:, :, a:b].reshape(rows, blocks * n), weight, preferred_el...  30.3 us
    all_to_all x4, local copies, waits for them, and re-layouts, fetch_adapter(): lax.all_to_all(mine, 'tenant', split_axis=2, concat_axis=0, tiled=True)  28.3 us
    all_gather x1, waiting for transfers between devices, shards(): whole = lax.all_gather(tokens, 'tenant', axis=1, tiled=True)  19.7 us
  transfers between devices with their start and end apart: 12, of which 8 were waited for; matrix products, arithmetic and copies ran while one was open for 36% of the time, Pallas kernels for 0%

profile of v1, /device:TPU:0, one launch (start us, length us, event | category | flops | bytes accessed | tf_op | source)
XLA Modules:
  0.0 561.7 jit_solution(6884710989709571941)
XLA Ops:
  8.5 4.0 copy.30
  12.5 4.9 reshape.172
  17.4 6.3 %all-to-all-start = ((bf16[4,2,40960]{2,1,0:T(2,128)(2,1)}), bf16[4,2,40960]{2,1,0:T(2,128)(2,1)S(1)}, u32[]{:S(2)}, u32[]{:S(2)}) async-start(bf16[4,2,40960]{2,1,0:T(2,128)(2,1)} %reshape.172), calls=%async_computation | async-start | bytes 1310720 | tf_op jit(solution)/shard_map/all_to_all | solution.py:23
  23.8 2.8 constant_dynamic-slice_fusion
  26.6 15.2 %copy.31 = bf16[2,32,14336]{1,0,2:T(2,128)(2,1)} copy(bf16[2,32,14336]{2,1,0:T(8,128)(2,1)} %constant_dynamic-slice_fusion) | data formatting | bytes 3670016
  41.9 9.4 %reshape.174 = bf16[4,2,114688]{2,1,0:T(2,128)(2,1)} reshape(bf16[14336,2,32]{2,1,0:T(2,128)(2,1)} %bitcast.66) | data formatting | bytes 3670016
  51.3 5.1 all-to-all-start.1
  56.3 2.6 reshape.173
  59.0 6.2 %copy.28 = bf16[2,32,4,1280]{3,2,1,0:T(4,128)(2,1)S(1)} copy(bf16[2,32,4,1280]{1,0,3,2:T(2,128)(2,1)} %bitcast.71) | data formatting | bytes 1310720 | tf_op jit(solution)/shard_map/all_to_all | solution.py:23
  66.2 32.3 %all-to-all-done.1 = bf16[4,2,114688]{2,1,0:T(2,128)(2,1)} async-done(((bf16[4,2,114688]{2,1,0:T(2,128)(2,1)}), bf16[4,2,114688]{2,1,0:T(2,128)(2,1)}, u32[]{:S(2)}, u32[]{:S(2)}) %all-to-all-start.1) | async-done | bytes 1835040 | tf_op jit(solution)/shard_map/all_to_all | solution.py:23
  98.5 6.9 %reshape.175 = bf16[14336,2,32]{2,1,0:T(2,128)(2,1)} reshape(bf16[4,2,114688]{2,1,0:T(2,128)(2,1)} %all-to-all-done.1) | data formatting | bytes 3670016
  105.4 18.1 %copy.29 = bf16[2,32,4,3584]{3,2,1,0:T(4,128)(2,1)} copy(bf16[2,32,4,3584]{1,0,3,2:T(2,128)(2,1)} %bitcast.67) | data formatting | bytes 3670016 | tf_op jit(solution)/shard_map/all_to_all | solution.py:23
  123.5 3.1 copy.24
  127.7 3.3 convolution_bitcast_fusion.1
  134.0 4.8 all-gather.10.cloned.1.call-done
  138.8 5.0 convolution_bitcast_fusion
  146.6 3.1 multiply_reduce_fusion.1
  149.8 30.7 %all-gather = f32[24,64,128]{2,1,0:T(8,128)S(1)} all-gather(f32[6,64,128]{2,1,0:T(8,128)S(1)} %pad_maximum_fusion.2), channel_id=2, replica_groups=mesh['fsdp'=4,'tenant'=4,'dp'=2] {'tenant'}, dimensions={0}, use_global_device_ids=true | all-gather | bytes 983040 | tf_op jit(solution)/shard_map/all_gather | solution.py:73
  183.8 1.8 mul.91
  185.5 1.8 mul.87
  187.3 3.6 fusion.11
  190.9 5.0 fusion.10
  195.9 8.3 %pad_maximum_fusion = f32[512,4864]{1,0:T(8,128)} fusion(f32[512,1280]{1,0:T(8,128)} %fusion.11, f32[512,3584]{1,0:T(8,128)} %fusion.10), kind=kLoop, calls=%fused_computation | loop fusion | flops 2490368 | bytes 19922944 | tf_op jit(solution)/shard_map/concatenate | solution.py:81
  204.2 2.9 slice.28
  207.2 3.5 slice.26
  210.7 19.7 %all-gather.12.cloned.1.call-done = bf16[384,5120]{1,0:T(8,128)(2,1)} async-done(((bf16[384,1280]{1,0:T(8,128)(2,1)}), bf16[384,5120]{1,0:T(8,128)(2,1)}) %all-gather.12.cloned.1.call-update) | async-done | bytes 3932176 | tf_op jit(solution)/shard_map/all_gather | solution.py:86
  230.5 2.9 copy.34
  233.8 2.0 copy.35
  237.4 11.5 %reduce-scatter.2.cloned.1.call-done = f32[256,4864]{1,0:T(8,128)} async-done(((f32[512,4864]{1,0:T(8,128)}), f32[256,4864]{1,0:T(8,128)}) %reduce-scatter.2.cloned.1.call-update) | async-done | bytes 4980752 | tf_op jit(solution)/shard_map/reduce_scatter | solution.py:82
  248.8 4.1 convert_element_type.69
  253.0 4.5 all-to-all-start.4
  257.5 6.6 %fusion.8 = f32[384,3584]{1,0:T(8,128)} fusion(bf16[384,512]{1,0:T(8,128)(2,1)S(1)} %mul.87, bf16[512,3584]{1,0:T(8,128)(2,1)} %bitcast.83), kind=kOutput, calls=%fused_computation.33 | convolution fusion | flops 1409286144 | bytes 9568256 | tf_op jit(solution)/shard_map/dot_general | solution.py:88
  264.1 92.3 %all-gather.16.cloned.1.call-done = bf16[2048,3584]{1,0:T(8,128)(2,1)} async-done(((bf16[256,3584]{1,0:T(8,128)(2,1)}), bf16[2048,3584]{1,0:T(8,128)(2,1)}) %all-gather.16.cloned.1.call-update) | async-done | bytes 14680080 | tf_op jit(solution)/shard_map/all_gather | solution.py:57
  356.4 9.5 %convolution_convert_fusion.1 = bf16[384,2048]{1,0:T(8,128)(2,1)S(1)} fusion(bf16[384,3584]{1,0:T(8,128)(2,1)S(1)} %copy-done, bf16[2048,3584]{1,0:T(8,128)(2,1)} %all-gather.16.cloned.1.call-done), kind=kOutput, calls=%fused_computation.9 | convolution fusion | flops 5637931008 | bytes 19005440 | tf_op jit(solution)/shard_map/dot_general | solution.py:13
  367.2 4.6 all-to-all-start.3
  371.9 3.1 reduce_sum.72
  375.0 95.7 %all-gather.14.cloned.1.call-done = bf16[3072,3584]{1,0:T(8,128)(2,1)} async-done(((bf16[384,3584]{1,0:T(8,128)(2,1)}), bf16[3072,3584]{1,0:T(8,128)(2,1)}) %all-gather.14.cloned.1.call-update) | async-done | bytes 22020112 | tf_op jit(solution)/shard_map/all_gather | solution.py:57
  470.6 14.1 %convolution_convert_fusion = bf16[384,3072]{1,0:T(8,128)(2,1)} fusion(bf16[384,3584]{1,0:T(8,128)(2,1)S(1)} %copy-done, bf16[3072,3584]{1,0:T(8,128)(2,1)} %all-gather.14.cloned.1.call-done), kind=kOutput, calls=%fused_computation.5 | convolution fusion | flops 8456896512 | bytes 27131904 | tf_op jit(solution)/shard_map/dot_general | solution.py:13
  484.7 3.2 copy.40
  487.9 4.7 all-to-all-start.2
  492.6 11.6 %fusion.9 = f32[384,3584]{1,0:T(8,128)} fusion(bf16[384,2048]{1,0:T(8,128)(2,1)S(1)} %bitcast.89, bf16[2048,3584]{1,0:T(8,128)(2,1)} %all-gather.16.cloned.1.call-done), kind=kOutput, calls=%fused_computation.34 | convolution fusion | flops 5637144576 | bytes 21757952 | tf_op jit(solution)/shard_map/dot_general | solution.py:101
  507.3 4.2 all-gather.18.cloned.1.call-done
  511.5 2.4 slice.36
  513.9 2.3 slice.37
  516.2 18.7 %fusion.1 = bf16[384,3584]{1,0:T(8,128)(2,1)} fusion(f32[384,3584]{1,0:T(8,128)} %fusion.9, f32[384,3584]{1,0:T(8,128)} %fusion.8, bf16[384,3072]{1,0:T(8,128)(2,1)S(1)} %bitcast.87, bf16[3072,3584]{1,0:T(8,128)(2,1)} %all-gather.14.cloned.1.call-done), kind=kOutput, calls=%fused_computation.3 | convolution fusion | flops 8459845632 | bytes 38141952 | tf_op jit(solution)/shard_map/dot_general | solution.py:101
  535.0 12.2 %all-to-all-done.2 = bf16[4,384,768]{2,1,0:T(8,128)(2,1)} async-done(((bf16[4,384,768]{2,1,0:T(8,128)(2,1)}), bf16[4,384,768]{2,1,0:T(8,128)(2,1)}, u32[]{:S(2)}, u32[]{:S(2)}) %all-to-all-start.2) | async-done | bytes 2359328 | tf_op jit(solution)/shard_map/all_to_all | solution.py:93
  547.2 2.1 convert_reduce_fusion
  549.9 2.0 pad_maximum_fusion.1
  (57 shorter events, 22.7 us)
Async XLA Ops:
  7.2 131.6 %copy-start = (bf16[384,3584]{1,0:T(8,128)(2,1)S(1)}, bf16[384,3584]{1,0:T(8,128)(2,1)}, u32[]{:S(2)}) copy-start(bf16[384,3584]{1,0:T(8,128)(2,1)} %param.13) | copy-start | bytes 8257540
  17.4 33.8 %all-to-all-start = ((bf16[4,2,40960]{2,1,0:T(2,128)(2,1)}), bf16[4,2,40960]{2,1,0:T(2,128)(2,1)S(1)}, u32[]{:S(2)}, u32[]{:S(2)}) async-start(bf16[4,2,40960]{2,1,0:T(2,128)(2,1)} %reshape.172), calls=%async_computation | async-start | bytes 1310720 | tf_op jit(solution)/shard_map/all_to_all | solution.py:23
  51.3 47.2 %all-to-all-start.1 = ((bf16[4,2,114688]{2,1,0:T(2,128)(2,1)}), bf16[4,2,114688]{2,1,0:T(2,128)(2,1)}, u32[]{:S(2)}, u32[]{:S(2)}) async-start(bf16[4,2,114688]{2,1,0:T(2,128)(2,1)} %reshape.174), calls=%async_computation.1 | async-start | bytes 3670016 | tf_op jit(solution)/shard_map/all_to_all | solution.py:23
  56.3 71.4 %all-gather.8.cloned.1.call-start = ((), (), s32[]{:S(2)}) async-start(), calls=%async_computation.6 | async-start | bytes 1966080 | tf_op jit(solution)/shard_map/all_gather | solution.py:24
  66.1 72.7 %all-gather.10.cloned.1.call-start = ((), (), s32[]{:S(2)}) async-start(), calls=%async_computation.7 | async-start | bytes 5505024 | tf_op jit(solution)/shard_map/all_gather | solution.py:24
  123.5 3.9 copy-start.6
  123.5 3.9 copy-start.7
  126.6 103.9 %all-gather.12.cloned.1.call-start = ((), (), s32[]{:S(2)}) async-start(), calls=%async_computation.8 | async-start | bytes 4915200 | tf_op jit(solution)/shard_map/all_gather | solution.py:86
  127.3 121.5 %reduce-scatter.2.cloned.1.call-start = ((), (), s32[]{:S(2)}) async-start(), calls=%async_computation.11 | async-start | bytes 14942208 | tf_op jit(solution)/shard_map/reduce_scatter | solution.py:82
  204.2 152.2 %all-gather.16.cloned.1.call-start = ((), (), s32[]{:S(2)}) async-start(), calls=%async_computation.10 | async-start | bytes 16515072 | tf_op jit(solution)/shard_map/all_gather | solution.py:57
  207.2 263.5 %all-gather.14.cloned.1.call-start = ((), (), s32[]{:S(2)}) async-start(), calls=%async_computation.9 | async-start | bytes 24772608 | tf_op jit(solution)/shard_map/all_gather | solution.py:57
  253.0 114.2 %all-to-all-start.4 = ((bf16[4,64,4864]{2,1,0:T(8,128)(2,1)}), bf16[4,64,4864]{2,1,0:T(8,128)(2,1)}, u32[]{:S(2)}, u32[]{:S(2)}) async-start(bf16[4,64,4864]{2,1,0:T(8,128)(2,1)} %bitcast.72), calls=%async_computation.5 | async-start | bytes 4980736 | tf_op jit(solution)/shard_map/all_to_all | solution.py:29
  367.2 120.7 %all-to-all-start.3 = ((bf16[4,384,512]{2,1,0:T(8,128)(2,1)}), bf16[4,384,512]{2,1,0:T(8,128)(2,1)}, u32[]{:S(2)}, u32[]{:S(2)}) async-start(bf16[4,384,512]{2,1,0:T(8,128)(2,1)} %bitcast.78), calls=%async_computation.3 | async-start | bytes 3145728 | tf_op jit(solution)/shard_map/all_to_all | solution.py:93
  371.8 139.7 %all-gather.18.cloned.1.call-start = ((), (), s32[]{:S(2)}) async-start(), calls=%async_computation.12 | async-start | bytes 3112960 | tf_op jit(solution)/shard_map/all_gather | solution.py:33
  487.9 4.7 copy-start.4
  487.9 59.2 %all-to-all-start.2 = ((bf16[4,384,768]{2,1,0:T(8,128)(2,1)}), bf16[4,384,768]{2,1,0:T(8,128)(2,1)}, u32[]{:S(2)}, u32[]{:S(2)}) async-start(bf16[4,384,768]{2,1,0:T(8,128)(2,1)} %bitcast.63), calls=%async_computation.2 | async-start | bytes 4718592 | tf_op jit(solution)/shard_map/all_to_all | solution.py:93
  511.5 2.4 copy-start.2
  513.9 2.3 copy-start.3
  551.9 1.3 copy-start.5
  551.9 2.9 copy-start.1
Sparse Core Ops, SparseCore 0:
  66.2 10.8 all-gather.7
  126.7 12.0 all-gather.9
  140.3 90.0 all-gather.11
  232.6 16.1 reduce-scatter.1
  250.6 105.7 all-gather.15
  358.7 111.8 all-gather.13
  473.1 38.4 all-gather.17
